TPU v7x, 32 devices: a whole 2x2x4 slice. The times are simulated.
32 devices in a mesh: dp: 8 (over y, x, core), tensor: 4 (over z).
Axes of the slice: x: 2, y: 2, z: 4, core: 2. Of those that a mesh axis runs over, the one named last changes fastest.
Arguments:
- hidden: bfloat16 [1024, 8192], P('dp')
- q_weight: float32 [8192, 4096], P(('dp', 'tensor')), may hold values from -0.0625 to 0.0625
- k_weight: float32 [8192, 1024], P(('dp', 'tensor')), may hold values from -0.0625 to 0.0625
- v_weight: float32 [8192, 1024], P(('dp', 'tensor')), may hold values from -0.0625 to 0.0625
- o_weight: float32 [8192, 4096], P(('dp', 'tensor')), may hold values from -0.09375 to 0.09375
- input_gain: float32 [8192], replicated, may hold values from 0.25 to 1.75
- post_gain: float32 [8192], replicated, may hold values from 0.25 to 1.75
- key_cache: bfloat16 [1024, 64, 8, 128], P('dp', None, 'tensor'), may hold values from -1000 to 1000
- value_cache: bfloat16 [1024, 64, 8, 128], P('dp', None, 'tensor'), may hold values from -6 to 6
- lengths: int32 [1024], P('dp'), may hold values from 1 to 64
Outputs:
- new_hidden: bfloat16 [1024, 8192], P('dp')
- normed: bfloat16 [1024, 8192], P('dp')
- fresh_token_keys: bfloat16 [1024, 8, 128], P('dp', 'tensor')
- new_values: bfloat16 [1024, 8, 128], P('dp', 'tensor')
All inputs are finite; a program needn't handle non-finite values.
Results may differ from a plain program's by a relative error of at most 0.012.
The roundings to bfloat16 on the way count: a program that leaves them out, or rounds other values in their place, can miss the bound.
Values may be sent and summed in bfloat16 or wider, within the bound.
A program may use at most 128 MiB of HBM per device.

v0:
```python
import math
import jax
import jax.numpy as jnp
from jax import lax
from jax.sharding import PartitionSpec as P

HEADS = 32
KV_HEADS = 8
HEAD_DIM = 128
epsilon = 1e-05
rope_base = 500000.0


def rms_gain(values, gain_vector):
    mean_square = jnp.mean(values * values, axis=-1, keepdims=True)
    return values * lax.rsqrt(mean_square + epsilon) * gain_vector


def rotate(values, positions):
    half_dim = values.shape[-1] // 2
    index_row = jnp.arange(half_dim, dtype=jnp.float32)
    frequency = jnp.exp(-math.log(rope_base) * index_row / half_dim)
    angle = positions.astype(jnp.float32)[:, None, None] * frequency[None, None, :]
    first_half = values[..., :half_dim]
    second_half = values[..., half_dim:]
    return jnp.concatenate(
        [
            first_half * jnp.cos(angle) - second_half * jnp.sin(angle),
            second_half * jnp.cos(angle) + first_half * jnp.sin(angle),
        ],
        axis=-1,
    )


def attend(query_b, fresh_token_keys, new_values, key_cache, value_cache, lengths):
    row_count, kv_count = (fresh_token_keys.shape[0], fresh_token_keys.shape[1])
    grouped_heads = query_b.reshape(row_count, kv_count, -1, HEAD_DIM)
    reciprocal_root = 1.0 / math.sqrt(HEAD_DIM)
    scores = (
        jnp.einsum("bkgd,blkd->bkgl", grouped_heads, key_cache, preferred_element_type=jnp.float32)
        * reciprocal_root
    )
    self_token_score = (
        jnp.einsum(
            "lfxa,lfa->lfx", grouped_heads, fresh_token_keys, preferred_element_type=jnp.float32
        )
        * reciprocal_root
    )
    visible = jnp.arange(key_cache.shape[1], dtype=jnp.int32)[None, :] < lengths[:, None]
    scores = jnp.where(visible[:, None, None, :], scores, -jnp.inf)
    largest = jnp.maximum(jnp.max(scores, axis=-1), self_token_score)
    kept_exp = jnp.exp(scores - largest[..., None])
    own_exp = jnp.exp(self_token_score - largest)
    softmax_divisor = jnp.sum(kept_exp, axis=-1) + own_exp
    weights_kept = (kept_exp / softmax_divisor[..., None]).astype(jnp.bfloat16)
    own_weight = (own_exp / softmax_divisor).astype(jnp.bfloat16)
    attended = jnp.einsum(
        "bkgl,blkd->bkgd", weights_kept, value_cache, preferred_element_type=jnp.float32
    )
    attended = (
        attended
        + own_weight.astype(jnp.float32)[..., None] * new_values.astype(jnp.float32)[:, :, None, :]
    )
    return attended.reshape(row_count, -1).astype(jnp.bfloat16)


def shards(
    hidden,
    q_weight,
    k_weight,
    v_weight,
    o_weight,
    input_gain,
    post_gain,
    key_cache,
    value_cache,
    lengths,
):
    tensor_size = lax.axis_size("tensor")
    row_count = hidden.shape[0]
    heads_here = HEADS // tensor_size
    kv_here = KV_HEADS // tensor_size
    w_query, w_key, value_matrix, w_out = (
        lax.all_to_all(
            q_weight.astype(jnp.bfloat16), "tensor", split_axis=1, concat_axis=0, tiled=True
        ),
        lax.all_to_all(
            k_weight.astype(jnp.bfloat16), "tensor", split_axis=1, concat_axis=0, tiled=True
        ),
        lax.all_to_all(
            v_weight.astype(jnp.bfloat16), "tensor", split_axis=1, concat_axis=0, tiled=True
        ),
        lax.all_to_all(
            o_weight.astype(jnp.bfloat16), "tensor", split_axis=1, concat_axis=0, tiled=True
        ),
    )
    normal_in = rms_gain(hidden.astype(jnp.float32), input_gain).astype(jnp.bfloat16)
    portions = (
        lax.all_gather(w_query, "dp", axis=0, tiled=True),
        lax.all_gather(w_key, "dp", axis=0, tiled=True),
        lax.all_gather(value_matrix, "dp", axis=0, tiled=True),
    )
    query, key_part, value_part = tuple(
        (jnp.dot(normal_in, portion, preferred_element_type=jnp.float32) for portion in portions)
    )
    query_b = rotate(query.reshape(row_count, heads_here, HEAD_DIM), lengths).astype(jnp.bfloat16)
    fresh_token_keys = rotate(key_part.reshape(row_count, kv_here, HEAD_DIM), lengths).astype(
        jnp.bfloat16
    )
    new_values = value_part.reshape(row_count, kv_here, HEAD_DIM).astype(jnp.bfloat16)
    attended = attend(query_b, fresh_token_keys, new_values, key_cache, value_cache, lengths)
    partial_value = lax.dot_general(
        attended,
        lax.all_gather(w_out, "dp", axis=0, tiled=True),
        (((1,), (1,)), ((), ())),
        preferred_element_type=jnp.float32,
    )
    mixed = lax.psum(partial_value.astype(jnp.bfloat16), "tensor").astype(jnp.float32)
    residual = hidden.astype(jnp.float32) + mixed
    new_hidden = residual.astype(jnp.bfloat16)
    normed = rms_gain(residual, post_gain).astype(jnp.bfloat16)
    return (new_hidden, normed, fresh_token_keys, new_values)


def solution(mesh):
    in_specs = (
        P("dp", None),
        P(("dp", "tensor"), None),
        P(("dp", "tensor"), None),
        P(("dp", "tensor"), None),
        P(("dp", "tensor"), None),
        P(),
        P(),
        P("dp", None, "tensor", None),
        P("dp", None, "tensor", None),
        P("dp"),
    )
    out_specs = (P("dp", None), P("dp", None), P("dp", "tensor", None), P("dp", "tensor", None))
    return jax.shard_map(shards, mesh=mesh, in_specs=in_specs, out_specs=out_specs, check_vma=False)
```

profile of v0, /device:TPU:0, one launch (start us, length us, event | category | flops | bytes accessed | tf_op | source)
XLA Modules:
  0.0 400.4 jit_solution(6438174233000839104)
XLA Ops:
  7.2 0.0 all-gather.7.cloned.1.call-start
  7.2 1.5 copy.44
  8.7 20.6 %all_to_all.76 = bf16[256,4,256]{0,2,1:T(8,128)(2,1)S(1)} all-to-all(bf16[256,4,256]{0,2,1:T(8,128)(2,1)S(1)} %bitcast.47), channel_id=1, replica_groups=mesh['dp'=8,'tensor'=4] {'tensor'}, dimensions={1} | all-to-all | bytes 1048576 | tf_op jit(solution)/shard_map/all_to_all | solution.py:87
  29.4 1.0 copy.45
  30.4 0.0 all-gather.9.cloned.1.call-start
  30.5 0.2 copy.52
  30.7 16.6 %all_to_all.77 = bf16[256,4,256]{0,2,1:T(8,128)(2,1)S(1)} all-to-all(bf16[256,4,256]{0,2,1:T(8,128)(2,1)S(1)} %bitcast.48), channel_id=1, replica_groups=mesh['dp'=8,'tensor'=4] {'tensor'}, dimensions={1} | all-to-all | bytes 1048576 | tf_op jit(solution)/shard_map/all_to_all | solution.py:90
  47.3 1.0 copy.53
  48.3 0.0 all-gather.5.cloned.1.call-start
  48.4 4.0 copy.41
  52.3 50.3 %all_to_all.78 = bf16[256,4,1024]{0,2,1:T(8,128)(2,1)} all-to-all(bf16[256,4,1024]{0,2,1:T(8,128)(2,1)S(1)} %bitcast.40), channel_id=1, replica_groups=mesh['dp'=8,'tensor'=4] {'tensor'}, dimensions={1} | all-to-all | bytes 4194304 | tf_op jit(solution)/shard_map/all_to_all | solution.py:84
  102.6 3.9 copy.42
  106.6 0.0 all-gather.11.cloned.1.call-start
  106.6 3.8 copy.54
  110.4 50.5 %all_to_all.79 = bf16[256,4,1024]{0,2,1:T(8,128)(2,1)} all-to-all(bf16[256,4,1024]{0,2,1:T(8,128)(2,1)S(1)} %bitcast.41), channel_id=1, replica_groups=mesh['dp'=8,'tensor'=4] {'tensor'}, dimensions={1} | all-to-all | bytes 4194304 | tf_op jit(solution)/shard_map/all_to_all | solution.py:93
  160.9 4.1 %copy.55 = bf16[4,256,1024]{2,1,0:T(8,128)(2,1)} copy(bf16[4,256,1024]{1,2,0:T(8,128)(2,1)} %bitcast.45) | data formatting | bytes 4194304 | tf_op jit(solution)/shard_map/all_to_all | solution.py:93
  165.0 0.2 all-reduce.2.cloned.1.call-start
  165.3 0.5 fusion
  165.8 0.7 iota_compare_fusion
  166.5 0.3 multiply_cosine_fusion
  166.8 0.0 all-gather.7.cloned.1.call-done
  166.8 3.0 fusion.29
  169.9 0.1 reshape.139
  170.0 2.9 convolution_convert_fusion.1
  173.0 0.7 convert_element_type.81
  173.7 0.3 subtract_convert_fusion.1
  174.0 0.2 fusion.38
  174.2 22.8 %all-gather.5.cloned.1.call-done = bf16[8192,1024]{1,0:T(8,128)(2,1)} async-done(((bf16[1024,1024]{1,0:T(8,128)(2,1)}), bf16[8192,1024]{1,0:T(8,128)(2,1)}) %all-gather.5.cloned.1.call-update) | async-done | bytes 16777232 | tf_op jit(solution)/shard_map/all_gather | solution.py:99
  197.0 8.1 %convolution_bitcast_fusion = f32[16,8,8,128]{3,1,2,0:T(8,128)S(1)} fusion(bf16[8192,1024]{1,0:T(8,128)(2,1)} %all-gather.5.cloned.1.call-done, bf16[128,8192]{1,0:T(8,128)(2,1)S(1)} %copy-done, f32[8192]{0:T(1024)S(1)} %copy-done.6, f32[128]{0:T(128)S(1)} %add_rsqrt_fusion.1), kind=kOutput, calls=%fused_computation.16 | convolution fusion | flops 2151677952 | bytes 19431936 | tf_op jit(solution)/shard_map/dot_general | solution.py:104
  205.1 0.1 copy.58
  205.2 0.3 subtract_convert_fusion
  205.5 0.5 fusion.23
  206.0 0.1 copy.57
  206.1 5.5 %fusion.32 = (f32[128,2,4]{2,1,0:T(2,128)S(1)}, f32[128,2,4,64]{3,2,1,0:T(4,128)S(1)}) fusion(bf16[128,64,2,128]{3,2,1,0:T(2,128)(2,1)} %param.17, bf16[128,2,4,64]{3,2,1,0:T(4,128)(2,1)S(1)} %bitcast.56, bf16[128,2,4,64]{3,2,1,0:T(4,128)(2,1)S(1)} %bitcast.54, pred[128,64]{1,0:T(8,128)(4,1)} %iota_compare_fusion), kind=kOutput, calls=%fused_computation.46 | convolution fusion | flops 17497088 | bytes 4730880 | tf_op jit(solution)/shard_map/bkgd,blkd->bkgl/dot_general | solution.py:40
  211.6 0.1 copy.46
  211.7 0.2 copy.47
  211.9 0.8 fusion.20
  212.7 0.1 copy.48
  212.8 0.2 copy.49
  213.0 0.2 copy.51
  213.1 3.5 fusion.14
  216.6 0.2 convert_element_type.83
  216.8 72.3 %all-gather.11.cloned.1.call-done = bf16[8192,1024]{1,0:T(8,128)(2,1)} async-done(((bf16[1024,1024]{1,0:T(8,128)(2,1)}), bf16[8192,1024]{1,0:T(8,128)(2,1)}) %all-gather.11.cloned.1.call-update) | async-done | bytes 16777232 | tf_op jit(solution)/shard_map/all_gather | solution.py:114
  289.1 12.9 %convolution_convert_fusion = bf16[128,8192]{1,0:T(8,128)(2,1)} fusion(bf16[128,1024]{1,0:T(8,128)(2,1)S(1)} %convert_element_type.83, bf16[8192,1024]{1,0:T(8,128)(2,1)} %all-gather.11.cloned.1.call-done), kind=kOutput, calls=%fused_computation | convolution fusion | flops 2148532224 | bytes 19136512 | tf_op jit(solution)/shard_map/dot_general | solution.py:112
  302.0 0.8 pad_maximum_fusion.1
  302.8 85.5 %all-reduce.2.cloned.1.call-done = bf16[128,8192]{1,0:T(8,128)(2,1)} async-done(((bf16[128,8192]{1,0:T(8,128)(2,1)}), bf16[128,8192]{1,0:T(8,128)(2,1)}) %all-reduce.2.cloned.1.call-update) | async-done | bytes 2097168 | tf_op jit(solution)/shard_map/psum | solution.py:118
  388.3 2.5 multiply_reduce_fusion
  390.8 3.0 multiply_convert_fusion
  (27 shorter events, 0.2 us)
Async XLA Ops:
  7.2 23.3 %copy-start.2 = (f32[256,1024]{1,0:T(8,128)S(1)}, f32[256,1024]{1,0:T(8,128)}, u32[]{:S(2)}) copy-start(f32[256,1024]{1,0:T(8,128)} %param.13) | copy-start | bytes 3145732
  7.2 159.7 %all-gather.7.cloned.1.call-start = ((), (), s32[]{:S(2)}) async-start(), calls=%async_computation.5 | async-start | bytes 4718592 | tf_op jit(solution)/shard_map/all_gather | solution.py:100
  30.4 139.6 %all-gather.9.cloned.1.call-start = ((), (), s32[]{:S(2)}) async-start(), calls=%async_computation.6 | async-start | bytes 4718592 | tf_op jit(solution)/shard_map/all_gather | solution.py:101
  48.3 148.7 %all-gather.5.cloned.1.call-start = ((), (), s32[]{:S(2)}) async-start(), calls=%async_computation.4 | async-start | bytes 18874368 | tf_op jit(solution)/shard_map/all_gather | solution.py:99
  106.6 182.5 %all-gather.11.cloned.1.call-start = ((), (), s32[]{:S(2)}) async-start(), calls=%async_computation.7 | async-start | bytes 18874368 | tf_op jit(solution)/shard_map/all_gather | solution.py:114
  160.9 4.4 %copy-start.5 = (s32[128]{0:T(128)S(1)}, s32[128]{0:T(128)}, u32[]{:S(2)}) copy-start(s32[128]{0:T(128)} %param.19) | copy-start | bytes 1540
  160.9 4.4 %copy-start = (bf16[128,8192]{1,0:T(8,128)(2,1)S(1)}, bf16[128,8192]{1,0:T(8,128)(2,1)}, u32[]{:S(2)}) copy-start(bf16[128,8192]{1,0:T(8,128)(2,1)} %param.10) | copy-start | bytes 6291460
  160.9 5.9 %copy-start.6 = (f32[8192]{0:T(1024)S(1)}, f32[8192]{0:T(1024)}, u32[]{:S(2)}) copy-start(f32[8192]{0:T(1024)} %param.15) | copy-start | bytes 98308
  165.0 223.3 %all-reduce.2.cloned.1.call-start = ((), (), s32[]{:S(2)}) async-start(), calls=%async_computation.8 | async-start | bytes 4194304 | tf_op jit(solution)/shard_map/psum | solution.py:118
  173.0 32.2 %copy-start.3 = (bf16[128,2,128]{2,1,0:T(2,128)(2,1)}, bf16[128,2,128]{2,1,0:T(2,128)(2,1)S(1)}, u32[]{:S(2)}) copy-start(bf16[128,2,128]{2,1,0:T(2,128)(2,1)S(1)} %convert_element_type.80) | copy-start | bytes 196612
  302.0 88.8 %copy-start.4 = (f32[8192]{0:T(1024)S(1)}, f32[8192]{0:T(1024)}, u32[]{:S(2)}) copy-start(f32[8192]{0:T(1024)} %param.16) | copy-start | bytes 98308
  388.3 2.5 copy-start.1
Sparse Core Ops, SparseCore 0:
  30.5 35.7 all-gather.6
  68.2 36.5 all-gather.8
  107.2 89.7 all-gather.4
  199.3 89.7 all-gather.10
  302.1 86.1 all-reduce.1
where the time goes:
time: 401 us; the launch traced here: 400 us
  waiting for transfers between devices  181 us (45%)
  blocking collectives  138 us (34%)
  matrix products  36.5 us (9%)
  local copies, waits for them, and re-layouts  20.6 us (5%)
  between operations  14 us (3%)
  other arithmetic  10.1 us (3%)
    psum x1, waiting for transfers between devices, shards(): lax.psum(partial_value.astype(jnp.bfloat16), 'tensor').astype(jnp.float32)  85.5 us
    all_gather x1, waiting for transfers between devices, shards(): lax.all_gather(w_out, 'dp', axis=0, tiled=True)  72.3 us
    all_to_all x1, blocking collectives, shards(): lax.all_to_all(o_weight.astype(jnp.bfloat16), 'tensor', split_axis=1, con...  50.5 us
    all_to_all x1, blocking collectives, shards(): lax.all_to_all(q_weight.astype(jnp.bfloat16), 'tensor', split_axis=1, con...  50.3 us
    all_gather x1, waiting for transfers between devices, shards(): lax.all_gather(w_query, 'dp', axis=0, tiled=True)  22.8 us
    all_to_all x1, blocking collectives, shards(): lax.all_to_all(k_weight.astype(jnp.bfloat16), 'tensor', split_axis=1, con...  20.6 us
    all_to_all x1, blocking collectives, shards(): lax.all_to_all(v_weight.astype(jnp.bfloat16), 'tensor', split_axis=1, con...  16.6 us
    dot_general x3, matrix products, shards(): jnp.dot(normal_in, portion, preferred_element_type=jnp.float32)  14.1 us
  transfers between devices with their start and end apart: 5, of which 3 were waited for; matrix products, arithmetic and copies ran while one was open for 12% of the time, Pallas kernels for 0%

commit v1 on v0

--- a/solution.py
+++ b/solution.py
@@ -3,12 +3,22 @@
 import jax.numpy as jnp
 from jax import lax
 from jax.sharding import PartitionSpec as P
+from jax.lax import all_to_all, axis_size
 
 HEADS = 32
 KV_HEADS = 8
 HEAD_DIM = 128
 epsilon = 1e-05
 rope_base = 500000.0
+point_signs = lambda tile_in, named_axis: jnp.concatenate(
+    all_to_all(
+        jnp.stack(jnp.split(tile_in, axis_size(named_axis), axis=1)),
+        named_axis,
+        concat_axis=0,
+        split_axis=0,
+    ),
+    axis=0,
+)
 
 
 def rms_gain(values, gain_vector):
@@ -81,9 +91,7 @@
     heads_here = HEADS // tensor_size
     kv_here = KV_HEADS // tensor_size
     w_query, w_key, value_matrix, w_out = (
-        lax.all_to_all(
-            q_weight.astype(jnp.bfloat16), "tensor", split_axis=1, concat_axis=0, tiled=True
-        ),
+        point_signs(q_weight.astype(jnp.bfloat16), "tensor"),
         lax.all_to_all(
             k_weight.astype(jnp.bfloat16), "tensor", split_axis=1, concat_axis=0, tiled=True
         ),

time: 401 us -> 401 us (level)
  local copies, waits for them, and re-layouts: 20.6 us -> 12.9 us
  waiting for transfers between devices: 181 us -> 186 us
    all_gather x1, waiting for transfers between devices: 22.8 us -> 27.7 us  [shards(): lax.all_gather(w_query, 'dp', axis=0, tiled=True)]
    unnamed x19 -> x18, local copies, waits for them, and re-layouts: 9.56 us -> 5.65 us
  transfers between devices with their start and end apart: 5 -> 5, of which waited for: 3 -> 3; matrix products, arithmetic and copies ran while one was open for 12% -> 10% of each run, Pallas kernels for 0% -> 0%
where the time goes in v1:
time: 401 us; the launch traced here: 400 us
  waiting for transfers between devices  186 us (46%)
  blocking collectives  138 us (34%)
  matrix products  36.5 us (9%)
  between operations  14.1 us (4%)
  local copies, waits for them, and re-layouts  12.9 us (3%)
  other arithmetic  12.9 us (3%)
    psum x1, waiting for transfers between devices, shards(): lax.psum(partial_value.astype(jnp.bfloat16), 'tensor').astype(jnp.float32)  85.5 us
    all_gather x1, waiting for transfers between devices, shards(): lax.all_gather(w_out, 'dp', axis=0, tiled=True)  72.3 us
    all_to_all x1, blocking collectives, all_to_all(jnp.stack(jnp.split(tile_in, axis_size(named_axis), axis=1)),...  50.5 us
    all_to_all x1, blocking collectives, shards(): lax.all_to_all(o_weight.astype(jnp.bfloat16), 'tensor', split_axis=1, con...  50.4 us
    all_gather x1, waiting for transfers between devices, shards(): lax.all_gather(w_query, 'dp', axis=0, tiled=True)  27.7 us
    all_to_all x1, blocking collectives, shards(): lax.all_to_all(k_weight.astype(jnp.bfloat16), 'tensor', split_axis=1, con...  20.6 us
    all_to_all x1, blocking collectives, shards(): lax.all_to_all(v_weight.astype(jnp.bfloat16), 'tensor', split_axis=1, con...  16.6 us
    dot_general x3, matrix products, shards(): jnp.dot(normal_in, portion, preferred_element_type=jnp.float32)  14 us
  transfers between devices with their start and end apart: 5, of which 3 were waited for; matrix products, arithmetic and copies ran while one was open for 10% of the time, Pallas kernels for 0%

profile of v1, /device:TPU:0, one launch (start us, length us, event | category | flops | bytes accessed | tf_op | source)
XLA Modules:
  0.0 400.4 jit_solution(10106508403615806058)
XLA Ops:
  7.2 0.0 all-gather.7.cloned.1.call-start
  7.2 1.5 copy.38
  8.7 20.6 %all_to_all.62 = bf16[256,4,256]{0,2,1:T(8,128)(2,1)S(1)} all-to-all(bf16[256,4,256]{0,2,1:T(8,128)(2,1)S(1)} %bitcast.51), channel_id=1, replica_groups=mesh['dp'=8,'tensor'=4] {'tensor'}, dimensions={1} | all-to-all | bytes 1048576 | tf_op jit(solution)/shard_map/all_to_all | solution.py:95
  29.4 1.0 copy.39
  30.4 0.0 all-gather.9.cloned.1.call-start
  30.5 0.2 copy.46
  30.7 16.6 %all_to_all.63 = bf16[256,4,256]{0,2,1:T(8,128)(2,1)S(1)} all-to-all(bf16[256,4,256]{0,2,1:T(8,128)(2,1)S(1)} %bitcast.52), channel_id=1, replica_groups=mesh['dp'=8,'tensor'=4] {'tensor'}, dimensions={1} | all-to-all | bytes 1048576 | tf_op jit(solution)/shard_map/all_to_all | solution.py:98
  47.3 1.0 copy.47
  48.3 0.0 all-gather.5.cloned.1.call-start
  48.3 2.5 convert_element_type.72
  50.8 0.2 slice_bitcast_fusion.3
  51.0 0.3 pad_maximum_fusion
  51.3 50.5 %all_to_all.64 = bf16[4,256,1024]{2,1,0:T(8,128)(2,1)} all-to-all(bf16[4,256,1024]{2,1,0:T(8,128)(2,1)S(1)} %pad_maximum_fusion), channel_id=1, replica_groups=mesh['dp'=8,'tensor'=4] {'tensor'}, dimensions={0} | all-to-all | bytes 4194304 | tf_op jit(solution)/shard_map/all_to_all | solution.py:14
  101.8 0.0 all-gather.11.cloned.1.call-start
  101.8 3.8 copy.48
  105.7 50.4 %all_to_all.65 = bf16[256,4,1024]{0,2,1:T(8,128)(2,1)} all-to-all(bf16[256,4,1024]{0,2,1:T(8,128)(2,1)S(1)} %bitcast.46), channel_id=1, replica_groups=mesh['dp'=8,'tensor'=4] {'tensor'}, dimensions={1} | all-to-all | bytes 4194304 | tf_op jit(solution)/shard_map/all_to_all | solution.py:101
  156.1 4.1 %copy.49 = bf16[4,256,1024]{2,1,0:T(8,128)(2,1)} copy(bf16[4,256,1024]{1,2,0:T(8,128)(2,1)} %bitcast.49) | data formatting | bytes 4194304 | tf_op jit(solution)/shard_map/all_to_all | solution.py:101
  160.2 0.2 all-reduce.2.cloned.1.call-start
  160.5 0.5 fusion
  161.0 0.7 iota_compare_fusion
  161.7 0.3 multiply_cosine_fusion
  162.0 2.9 fusion.29
  165.0 0.1 reshape.140
  165.1 2.9 convolution_convert_fusion.1
  168.1 0.7 convert_element_type.81
  168.8 0.3 subtract_convert_fusion.1
  169.1 0.2 fusion.38
  169.3 27.7 %all-gather.5.cloned.1.call-done = bf16[8192,1024]{1,0:T(8,128)(2,1)} async-done(((bf16[1024,1024]{1,0:T(8,128)(2,1)}), bf16[8192,1024]{1,0:T(8,128)(2,1)}) %all-gather.5.cloned.1.call-update) | async-done | bytes 16777232 | tf_op jit(solution)/shard_map/all_gather | solution.py:107
  197.0 8.1 %convolution_bitcast_fusion = f32[16,8,8,128]{3,1,2,0:T(8,128)S(1)} fusion(bf16[8192,1024]{1,0:T(8,128)(2,1)} %all-gather.5.cloned.1.call-done, bf16[128,8192]{1,0:T(8,128)(2,1)S(1)} %copy-done, f32[8192]{0:T(1024)S(1)} %copy-done.6, f32[128]{0:T(128)S(1)} %add_rsqrt_fusion.1), kind=kOutput, calls=%fused_computation.17 | convolution fusion | flops 2151677952 | bytes 19431936 | tf_op jit(solution)/shard_map/dot_general | solution.py:112
  205.1 0.1 copy.52
  205.2 0.3 subtract_convert_fusion
  205.5 0.5 fusion.23
  206.0 0.1 copy.51
  206.1 5.5 %fusion.32 = (f32[128,2,4]{2,1,0:T(2,128)S(1)}, f32[128,2,4,64]{3,2,1,0:T(4,128)S(1)}) fusion(bf16[128,64,2,128]{3,2,1,0:T(2,128)(2,1)} %param.17, bf16[128,2,4,64]{3,2,1,0:T(4,128)(2,1)S(1)} %bitcast.60, bf16[128,2,4,64]{3,2,1,0:T(4,128)(2,1)S(1)} %bitcast.58, pred[128,64]{1,0:T(8,128)(4,1)} %iota_compare_fusion), kind=kOutput, calls=%fused_computation.51 | convolution fusion | flops 17497088 | bytes 4730880 | tf_op jit(solution)/shard_map/bkgd,blkd->bkgl/dot_general | solution.py:50
  211.6 0.1 copy.40
  211.7 0.2 copy.41
  211.9 0.8 fusion.20
  212.7 0.1 copy.42
  212.8 0.2 copy.43
  213.0 0.2 copy.45
  213.1 3.5 fusion.14
  216.6 0.2 convert_element_type.83
  216.8 72.3 %all-gather.11.cloned.1.call-done = bf16[8192,1024]{1,0:T(8,128)(2,1)} async-done(((bf16[1024,1024]{1,0:T(8,128)(2,1)}), bf16[8192,1024]{1,0:T(8,128)(2,1)}) %all-gather.11.cloned.1.call-update) | async-done | bytes 16777232 | tf_op jit(solution)/shard_map/all_gather | solution.py:122
  289.0 12.9 %convolution_convert_fusion = bf16[128,8192]{1,0:T(8,128)(2,1)} fusion(bf16[128,1024]{1,0:T(8,128)(2,1)S(1)} %convert_element_type.83, bf16[8192,1024]{1,0:T(8,128)(2,1)} %all-gather.11.cloned.1.call-done), kind=kOutput, calls=%fused_computation | convolution fusion | flops 2148532224 | bytes 19136512 | tf_op jit(solution)/shard_map/dot_general | solution.py:120
  302.0 0.8 pad_maximum_fusion.2
  302.8 85.5 %all-reduce.2.cloned.1.call-done = bf16[128,8192]{1,0:T(8,128)(2,1)} async-done(((bf16[128,8192]{1,0:T(8,128)(2,1)}), bf16[128,8192]{1,0:T(8,128)(2,1)}) %all-reduce.2.cloned.1.call-update) | async-done | bytes 2097168 | tf_op jit(solution)/shard_map/psum | solution.py:126
  388.3 2.5 multiply_reduce_fusion
  390.8 3.0 multiply_convert_fusion
  (28 shorter events, 0.2 us)
Async XLA Ops:
  7.2 23.3 %copy-start.2 = (f32[256,1024]{1,0:T(8,128)S(1)}, f32[256,1024]{1,0:T(8,128)}, u32[]{:S(2)}) copy-start(f32[256,1024]{1,0:T(8,128)} %param.13) | copy-start | bytes 3145732
  7.2 154.8 %all-gather.7.cloned.1.call-start = ((), (), s32[]{:S(2)}) async-start(), calls=%async_computation.5 | async-start | bytes 4718592 | tf_op jit(solution)/shard_map/all_gather | solution.py:108
  30.4 134.7 %all-gather.9.cloned.1.call-start = ((), (), s32[]{:S(2)}) async-start(), calls=%async_computation.6 | async-start | bytes 4718592 | tf_op jit(solution)/shard_map/all_gather | solution.py:109
  48.3 148.7 %all-gather.5.cloned.1.call-start = ((), (), s32[]{:S(2)}) async-start(), calls=%async_computation.4 | async-start | bytes 18874368 | tf_op jit(solution)/shard_map/all_gather | solution.py:107
  101.8 187.3 %all-gather.11.cloned.1.call-start = ((), (), s32[]{:S(2)}) async-start(), calls=%async_computation.7 | async-start | bytes 18874368 | tf_op jit(solution)/shard_map/all_gather | solution.py:122
  156.1 4.4 %copy-start.5 = (s32[128]{0:T(128)S(1)}, s32[128]{0:T(128)}, u32[]{:S(2)}) copy-start(s32[128]{0:T(128)} %param.19) | copy-start | bytes 1540
  156.1 4.4 %copy-start = (bf16[128,8192]{1,0:T(8,128)(2,1)S(1)}, bf16[128,8192]{1,0:T(8,128)(2,1)}, u32[]{:S(2)}) copy-start(bf16[128,8192]{1,0:T(8,128)(2,1)} %param.10) | copy-start | bytes 6291460
  156.1 5.9 %copy-start.6 = (f32[8192]{0:T(1024)S(1)}, f32[8192]{0:T(1024)}, u32[]{:S(2)}) copy-start(f32[8192]{0:T(1024)} %param.15) | copy-start | bytes 98308
  160.2 228.1 %all-reduce.2.cloned.1.call-start = ((), (), s32[]{:S(2)}) async-start(), calls=%async_computation.8 | async-start | bytes 4194304 | tf_op jit(solution)/shard_map/psum | solution.py:126
  168.1 37.1 %copy-start.3 = (bf16[128,2,128]{2,1,0:T(2,128)(2,1)}, bf16[128,2,128]{2,1,0:T(2,128)(2,1)S(1)}, u32[]{:S(2)}) copy-start(bf16[128,2,128]{2,1,0:T(2,128)(2,1)S(1)} %convert_element_type.80) | copy-start | bytes 196612
  302.0 88.8 %copy-start.4 = (f32[8192]{0:T(1024)S(1)}, f32[8192]{0:T(1024)}, u32[]{:S(2)}) copy-start(f32[8192]{0:T(1024)} %param.16) | copy-start | bytes 98308
  388.3 2.5 copy-start.1
Sparse Core Ops, SparseCore 0:
  30.5 35.6 all-gather.6
  68.7 36.5 all-gather.8
  107.2 89.7 all-gather.4
  199.3 89.7 all-gather.10
  302.1 86.1 all-reduce.1
